TPU v7x, 128 devices: a whole 4x4x4 slice. The times are simulated.
128 devices in a mesh: grp: 16 (over y_hi, z, core), tp: 8 (over y_lo, x).
Axes of the slice: x: 4, y: 4 (y_hi: 2, y_lo: 2; y = y_hi * 2 + y_lo), z: 4, core: 2. Of those that a mesh axis runs over, the one named last changes fastest.
Arguments:
- tokens: bfloat16 [16384, 8192], P('grp'), may hold values from -12 to 12
- joined_weight: bfloat16 [8192, 10240], P(('grp', 'tp')), may hold values from -1.14904852 to 1.14904852
- rollout_lengths: int32 [128], P('grp'), may hold values from 1 to 128
- prompt_of: int32 [128, 1], P('grp'), may hold values from 0 to 15
- score_weight: bfloat16 [8192], P('tp'), may hold values from -0.52734375 to 0.52734375
Outputs:
- attention: bfloat16 [16384, 8192], P('grp', 'tp')
- advantages: float32 [128], P('grp')
All inputs are finite; a program needn't handle non-finite values.
Results may differ from a plain program's by a relative error of at most 0.012.
The roundings to bfloat16 on the way count: a program that leaves them out, or rounds other values in their place, can miss the bound.
Values may be sent and summed in bfloat16 or wider, within the bound.
No kernel may reach another device: no remote copies, remote signals or barrier semaphores. Data moves between devices by JAX's collectives and lax.ppermute only.
A program may use at most 128 MiB of HBM per device.

v0:
```python
import jax
import jax.numpy as jnp
from jax import lax
from jax.sharding import PartitionSpec as P

QUERY_HEADS = 64
KV_HEAD_COUNT = 8
HEAD_SIZE = 128


def copy_for_each(shard, axis):
    copies = jnp.broadcast_to(shard, (lax.axis_size(axis), *shard.shape))
    return lax.all_to_all(copies, axis, split_axis=0, concat_axis=0, tiled=True)


def taken_together(shard, axis):
    return copy_for_each(shard, axis).sum(axis=0)


def together(arrays, axis):
    ends = [0]
    for a in arrays:
        ends.append(ends[-1] + a.size)
    running = taken_together(jnp.concatenate([a.ravel() for a in arrays]), axis)
    return tuple((running[b:e].reshape(a.shape) for a, b, e in zip(arrays, ends, ends[1:])))


def project_rows(block_rows, tokens):
    return jnp.dot(tokens, block_rows, preferred_element_type=jnp.float32)


def attend(joined_matrix, rollout_length_list):
    head_ratio = QUERY_HEADS // KV_HEAD_COUNT
    slot_index = joined_matrix.shape[0] // rollout_length_list.shape[0]
    groups = joined_matrix.shape[1] // ((head_ratio + 2) * HEAD_SIZE)
    reshaped_tensor = joined_matrix.reshape(
        rollout_length_list.shape[0], slot_index, groups, head_ratio + 2, HEAD_SIZE
    )
    queries = reshaped_tensor[:, :, :, :head_ratio, :]
    key_heads = reshaped_tensor[:, :, :, head_ratio, :]
    value_heads = reshaped_tensor[:, :, :, head_ratio + 1, :]
    scores = jnp.einsum(
        "rsgah,rtgh->rgast", queries, key_heads, preferred_element_type=jnp.float32
    ) * HEAD_SIZE ** (-0.5)
    positions = jnp.arange(slot_index)
    allowed = (positions[None, None, :] <= positions[None, :, None]) & (
        positions[None, None, :] < rollout_length_list[:, None, None]
    )
    scores = jnp.where(allowed[:, None, None], scores, jnp.float32(-1e30))
    peak = jnp.max(scores, axis=-1, keepdims=True)
    expo = jnp.exp(scores - peak)
    probs = (expo / jnp.sum(expo, axis=-1, keepdims=True)).astype(jnp.bfloat16)
    mixed = jnp.einsum("rgast,rtgh->rsgah", probs, value_heads, preferred_element_type=jnp.float32)
    return mixed.reshape(joined_matrix.shape[0], groups * head_ratio * HEAD_SIZE).astype(
        jnp.bfloat16
    )


def shards(tokens, joined_weight, rollout_lengths, prompt_of, score_weight):
    grp_count = lax.axis_size("grp")
    column_block = lax.all_to_all(joined_weight, "tp", split_axis=1, concat_axis=0, tiled=True)
    joined_matrix = project_rows(lax.all_gather(column_block, "grp", axis=0, tiled=True), tokens)
    attention = attend(joined_matrix.astype(jnp.bfloat16), rollout_lengths)
    partial_value = jnp.dot(attention, score_weight, preferred_element_type=jnp.float32)
    rollouts = rollout_lengths.shape[0]
    slot_index = tokens.shape[0] // rollouts
    valid = jnp.arange(slot_index)[None, :] < rollout_lengths[:, None]
    divisor_len = rollout_lengths.astype(jnp.float32)
    local_reward = (
        jnp.sum(
            jnp.where(valid, partial_value.reshape(rollouts, slot_index), jnp.float32(0.0)), axis=1
        )
        / divisor_len
    )
    rewards = taken_together(local_reward, "tp")
    onehot = (prompt_of == jnp.arange(grp_count)[None, :]).astype(jnp.float32)
    counts, totals, squares = together(
        (
            jnp.sum(onehot, axis=0),
            jnp.sum(onehot * rewards[:, None], axis=0),
            jnp.sum(onehot * (rewards * rewards)[:, None], axis=0),
        ),
        "grp",
    )
    divisor = jnp.maximum(counts, 1.0)
    average = totals / divisor
    spread = squares / divisor - average * average
    own_mean = jnp.sum(onehot * average[None, :], axis=1)
    own_var = jnp.sum(onehot * spread[None, :], axis=1)
    advantages = (rewards - own_mean) / jnp.sqrt(own_var + 0.25)
    return (attention, advantages)


def solution(mesh):
    return jax.shard_map(
        shards,
        mesh=mesh,
        in_specs=(P("grp", None), P(("grp", "tp"), None), P("grp"), P("grp", None), P("tp")),
        out_specs=(P("grp", "tp"), P("grp")),
        check_vma=False,
    )
```

profile of v0, /device:TPU:1, one launch (start us, length us, event | category | flops | bytes accessed | tf_op | source)
XLA Modules:
  0.0 233.0 jit_solution(10680021031263918509)
XLA Ops:
  7.2 0.0 copy-start
  7.2 0.0 copy-start.2
  7.2 0.0 all-gather.2.cloned.1.call-start
  7.2 1.4 copy.62
  8.6 23.4 %all_to_all.31 = bf16[64,8,1280]{2,0,1:T(8,128)(2,1)} all-to-all(bf16[64,8,1280]{2,0,1:T(8,128)(2,1)S(1)} %bitcast.80), channel_id=1, replica_groups=mesh['grp'=16,'tp'=8] {'tp'}, dimensions={1} | all-to-all | bytes 2621440 | tf_op jit(solution)/shard_map/all_to_all | solution.py:61
  32.1 0.0 all-gather.2.cloned.1.call-update
  32.1 0.0 copy-done
  32.1 0.0 copy-done.2
  32.2 0.1 iota_compare_fusion.2
  32.2 0.2 broadcast_and_fusion
  32.4 129.7 %all-gather.2.cloned.1.call-done = bf16[8192,1280]{1,0:T(8,128)(2,1)} async-done(((bf16[512,1280]{1,0:T(8,128)(2,1)}), bf16[8192,1280]{1,0:T(8,128)(2,1)}) %all-gather.2.cloned.1.call-update) | async-done | bytes 20971536 | tf_op jit(solution)/shard_map/all_gather | solution.py:62
  162.1 28.0 %convolution_convert_fusion = bf16[1024,1280]{1,0:T(8,128)(2,1)} fusion(bf16[1024,8192]{1,0:T(8,128)(2,1)} %param.5, bf16[8192,1280]{1,0:T(8,128)(2,1)} %all-gather.2.cloned.1.call-done), kind=kOutput, calls=%fused_computation.3 | convolution fusion | flops 21476147200 | bytes 40370176 | tf_op jit(solution)/shard_map/dot_general | solution.py:29
  190.1 3.0 %copy.39 = bf16[1024,1280]{0,1:T(8,128)(2,1)S(1)} copy(bf16[1024,1280]{1,0:T(8,128)(2,1)} %convolution_convert_fusion) | data formatting | bytes 5242880 | tf_op jit(solution)/shard_map/convert_element_type | solution.py:63
  193.1 0.6 copy.55
  193.8 1.5 slice.26
  195.3 0.2 copy.52
  195.5 3.3 %copy.53 = bf16[8,128,1,8,128]{4,1,3,0,2:T(8,128)(2,1)S(1)} copy(bf16[8,128,1,8,128]{1,0,4,3,2:T(8,128)(2,1)} %slice.26) | data formatting | bytes 4194304
  198.8 0.8 fusion.1
  199.6 1.2 fusion
  200.8 0.0 copy-start.1
  200.8 1.5 fusion.10
  202.4 0.4 fusion.17
  202.8 0.2 select_reduce_fusion.4
  203.0 8.8 %all_to_all.32 = f32[8,1,8]{2,1,0:T(1,128)S(1)} all-to-all(f32[8,1,8]{2,1,0:T(1,128)S(1)} %broadcast_in_dim.23), channel_id=1, replica_groups=mesh['grp'=16,'tp'=8] {'tp'}, dimensions={0} | all-to-all | bytes 512 | tf_op jit(solution)/shard_map/all_to_all | solution.py:13
  211.8 0.0 copy-done.1
  211.8 0.1 convert_reduce_fusion
  211.9 0.1 pad_maximum_fusion
  212.0 0.6 broadcast_in_dim.24
  212.6 5.7 %all-to-all-start.2 = ((f32[16,1,48]{2,1,0:T(1,128)}), f32[16,1,48]{2,1,0:T(1,128)S(1)}, u32[]{:S(2)}, u32[]{:S(2)}) async-start(f32[16,1,48]{2,1,0:T(1,128)} %broadcast_in_dim.24), calls=%async_computation.2 | async-start | bytes 16384 | tf_op jit(solution)/shard_map/all_to_all | solution.py:13
  218.3 2.8 %copy.44 = bf16[8,128,1,8,128]{4,3,1,0,2:T(8,128)(2,1)} copy(bf16[8,128,1,8,128]{1,4,3,0,2:T(8,128)(2,1)S(1)} %bitcast.77) | data formatting | bytes 4194304 | tf_op jit(solution)/shard_map/convert_element_type | solution.py:54
  221.1 3.5 %copy.61 = bf16[128,8,8,128]{3,1,2,0:T(8,128)(2,1)} copy(bf16[128,8,8,128]{3,2,1,0:T(8,128)(2,1)} %bitcast.78) | data formatting | bytes 4194304
  224.7 0.7 all-to-all-done.2
  225.3 0.1 multiply_subtract_fusion
  225.4 0.2 select_reduce_fusion.1
  225.6 0.5 rsqrt_multiply_fusion
  (8 shorter events, 0.1 us)
Async XLA Ops:
  7.2 24.9 %copy-start = (bf16[1024]{0:T(1024)(128)(2,1)S(1)}, bf16[1024]{0:T(1024)(128)(2,1)}, u32[]{:S(2)}) copy-start(bf16[1024]{0:T(1024)(128)(2,1)} %param.9) | copy-start | bytes 6148
  7.2 25.0 %copy-start.2 = (s32[8]{0:T(128)S(1)}, s32[8]{0:T(128)}, u32[]{:S(2)}) copy-start(s32[8]{0:T(128)} %param.7) | copy-start | bytes 100
  7.2 155.0 %all-gather.2.cloned.1.call-start = ((), (), s32[]{:S(2)}) async-start(), calls=%async_computation.3 | async-start | bytes 22282240 | tf_op jit(solution)/shard_map/all_gather | solution.py:62
  200.8 11.0 %copy-start.1 = (s32[8,1]{0,1:T(1,128)S(1)}, s32[8,1]{0,1:T(1,128)}, u32[]{:S(2)}) copy-start(s32[8,1]{0,1:T(1,128)} %param.8) | copy-start | bytes 100
  212.6 12.7 %all-to-all-start.2 = ((f32[16,1,48]{2,1,0:T(1,128)}), f32[16,1,48]{2,1,0:T(1,128)S(1)}, u32[]{:S(2)}, u32[]{:S(2)}) async-start(f32[16,1,48]{2,1,0:T(1,128)} %broadcast_in_dim.24), calls=%async_computation.2 | async-start | bytes 16384 | tf_op jit(solution)/shard_map/all_to_all | solution.py:13
Sparse Core Ops, SparseCore 0:
  32.2 129.8 all-gather.1
where the time goes:
time: 233 us
  waiting for transfers between devices  130 us (56%)
  blocking collectives  32.3 us (14%)
  matrix products  30.7 us (13%)
  local copies, waits for them, and re-layouts  17 us (7%)
  between operations  14.2 us (6%)
  starting transfers between devices  5.74 us (2%)
  other arithmetic  2.72 us (1%)
    all_gather x1, waiting for transfers between devices, shards(): lax.all_gather(column_block, 'grp', axis=0, tiled=True)  130 us
    dot_general x1, matrix products, project_rows(): return jnp.dot(tokens, block_rows, preferred_element_type=jnp.float32)  28 us
    all_to_all x1, blocking collectives, shards(): lax.all_to_all(joined_weight, 'tp', split_axis=1, concat_axis=0, tiled=True)  23.4 us
    all_to_all x1, blocking collectives, copy_for_each(): return lax.all_to_all(copies, axis, split_axis=0, concat_axis=0, tiled=True)  8.82 us
    unnamed x11, local copies, waits for them, and re-layouts  7.72 us
    all_to_all x1, starting transfers between devices, copy_for_each(): return lax.all_to_all(copies, axis, split_axis=0, concat_axis=0, tiled=True)  5.7 us
  transfers between devices with their start and end apart: 2, of which 2 were waited for; matrix products, arithmetic and copies ran while one was open for 3% of the time, Pallas kernels for 0%

commit v1 on v0

--- a/solution.py
+++ b/solution.py
@@ -59,7 +59,12 @@
 def shards(tokens, joined_weight, rollout_lengths, prompt_of, score_weight):
     grp_count = lax.axis_size("grp")
     column_block = lax.all_to_all(joined_weight, "tp", split_axis=1, concat_axis=0, tiled=True)
-    joined_matrix = project_rows(lax.all_gather(column_block, "grp", axis=0, tiled=True), tokens)
+    joined_matrix = project_rows(
+        jnp.concatenate(
+            lax.all_to_all(jnp.stack([column_block] * lax.axis_size("grp")), "grp", 0, 0), axis=0
+        ),
+        tokens,
+    )
     attention = attend(joined_matrix.astype(jnp.bfloat16), rollout_lengths)
     partial_value = jnp.dot(attention, score_weight, preferred_element_type=jnp.float32)
     rollouts = rollout_lengths.shape[0]

time: 233 us -> 436 us (1.87)
  waiting for transfers between devices: 130 us -> 322 us
  starting transfers between devices: 5.74 us -> 23.6 us
  between operations: 14.2 us -> 0.77 us
  local copies, waits for them, and re-layouts: 17 us -> 24.4 us
    all_to_all x0 -> x1, waiting for transfers between devices: none -> 322 us  [shards(): lax.all_to_all(jnp.stack([column_block] * lax.axis_size('grp')), 'grp', 0...]
    all_gather x1 -> x0, waiting for transfers between devices: 130 us -> none  [shards(): lax.all_gather(column_block, 'grp', axis=0, tiled=True)]
    all_to_all x0 -> x1, starting transfers between devices: none -> 9.58 us  [shards(): lax.all_to_all(jnp.stack([column_block] * lax.axis_size('grp')), 'grp', 0...]
    all_to_all x1, starting transfers between devices: 5.7 us -> 14 us  [copy_for_each(): return lax.all_to_all(copies, axis, split_axis=0, concat_axis=0, tiled=True)]
    another operation x0 -> x1, local copies, waits for them, and re-layouts: none -> 7.41 us  [shards(): jnp.stack([column_block] * lax.axis_size('grp'))]
  transfers between devices with their start and end apart: 2 -> 2, of which waited for: 2 -> 2; matrix products, arithmetic and copies ran while one was open for 3% -> 2% of each run, Pallas kernels for 0% -> 0%
where the time goes in v1:
time: 436 us; the launch traced here: 435 us
  waiting for transfers between devices  322 us (74%)
  blocking collectives  30.7 us (7%)
  matrix products  30.7 us (7%)
  local copies, waits for them, and re-layouts  24.4 us (6%)
  starting transfers between devices  23.6 us (5%)
    all_to_all x1, waiting for transfers between devices, shards(): lax.all_to_all(jnp.stack([column_block] * lax.axis_size('grp')), 'grp', 0...  322 us
    dot_general x1, matrix products, project_rows(): return jnp.dot(tokens, block_rows, preferred_element_type=jnp.float32)  28 us
    all_to_all x1, blocking collectives, shards(): lax.all_to_all(joined_weight, 'tp', split_axis=1, concat_axis=0, tiled=True)  23.3 us
    all_to_all x1, starting transfers between devices, copy_for_each(): return lax.all_to_all(copies, axis, split_axis=0, concat_axis=0, tiled=True)  14 us
    all_to_all x1, starting transfers between devices, shards(): lax.all_to_all(jnp.stack([column_block] * lax.axis_size('grp')), 'grp', 0...  9.58 us
  transfers between devices with their start and end apart: 2, of which 2 were waited for; matrix products, arithmetic and copies ran while one was open for 2% of the time, Pallas kernels for 0%

profile of v1, /device:TPU:1, one launch (start us, length us, event | category | flops | bytes accessed | tf_op | source)
XLA Modules:
  0.0 435.4 jit_solution(9763222292497925639)
XLA Ops:
  0.6 1.4 copy.62
  2.0 23.3 %all_to_all.33 = bf16[64,8,1280]{2,0,1:T(8,128)(2,1)S(1)} all-to-all(bf16[64,8,1280]{2,0,1:T(8,128)(2,1)S(1)} %bitcast.80), channel_id=1, replica_groups=mesh['grp'=16,'tp'=8] {'tp'}, dimensions={1} | all-to-all | bytes 2621440 | tf_op jit(solution)/shard_map/all_to_all | solution.py:61
  25.4 7.4 %stack.5 = bf16[16,512,1280]{2,1,0:T(8,128)(2,1)} broadcast(bf16[512,1280]{1,0:T(8,128)(2,1)S(1)} %bitcast.81), dimensions={1,2} | broadcast | bytes 22282240 | tf_op jit(solution)/shard_map/stack | solution.py:64
  32.8 0.0 copy-start
  32.8 0.0 copy-start.2
  32.8 9.6 %all-to-all-start.1 = ((bf16[16,512,1280]{2,1,0:T(8,128)(2,1)}), bf16[16,512,1280]{2,1,0:T(8,128)(2,1)}, u32[]{:S(2)}, u32[]{:S(2)}) async-start(bf16[16,512,1280]{2,1,0:T(8,128)(2,1)} %stack.5), calls=%async_computation.1 | async-start | bytes 41943040 | tf_op jit(solution)/shard_map/all_to_all | solution.py:64
  42.4 0.0 copy-done
  42.4 0.0 copy-done.2
  42.4 0.1 iota_compare_fusion.2
  42.5 0.2 broadcast_and_fusion
  42.7 321.8 %all-to-all-done.1 = bf16[16,512,1280]{2,1,0:T(8,128)(2,1)} async-done(((bf16[16,512,1280]{2,1,0:T(8,128)(2,1)}), bf16[16,512,1280]{2,1,0:T(8,128)(2,1)}, u32[]{:S(2)}, u32[]{:S(2)}) %all-to-all-start.1) | async-done | bytes 20971552 | tf_op jit(solution)/shard_map/all_to_all | solution.py:64
  364.5 28.0 %convolution_convert_fusion = bf16[1024,1280]{1,0:T(8,128)(2,1)} fusion(bf16[1024,8192]{1,0:T(8,128)(2,1)} %param.5, bf16[8192,1280]{1,0:T(8,128)(2,1)} %bitcast.2), kind=kOutput, calls=%fused_computation.3 | convolution fusion | flops 21476147200 | bytes 40370176 | tf_op jit(solution)/shard_map/dot_general | solution.py:29
  392.5 3.0 copy.39
  395.5 0.6 copy.55
  396.2 1.5 slice.26
  397.6 0.2 copy.52
  397.9 3.3 copy.53
  401.2 0.8 fusion.1
  402.0 1.2 fusion
  403.2 0.0 copy-start.1
  403.2 1.5 fusion.10
  404.8 0.4 fusion.17
  405.1 0.2 select_reduce_fusion.4
  405.3 7.4 %all_to_all.34 = f32[8,1,8]{2,1,0:T(1,128)S(1)} all-to-all(f32[8,1,8]{2,1,0:T(1,128)S(1)} %broadcast_in_dim.23), channel_id=1, replica_groups=mesh['grp'=16,'tp'=8] {'tp'}, dimensions={0} | all-to-all | bytes 512 | tf_op jit(solution)/shard_map/all_to_all | solution.py:13
  412.8 0.0 copy-done.1
  412.8 0.1 convert_reduce_fusion
  412.9 0.1 pad_maximum_fusion
  412.9 0.6 broadcast_in_dim.24
  413.6 14.0 %all-to-all-start.3 = ((f32[16,1,48]{2,1,0:T(1,128)}), f32[16,1,48]{2,1,0:T(1,128)S(1)}, u32[]{:S(2)}, u32[]{:S(2)}) async-start(f32[16,1,48]{2,1,0:T(1,128)} %broadcast_in_dim.24), calls=%async_computation.3 | async-start | bytes 16384 | tf_op jit(solution)/shard_map/all_to_all | solution.py:13
  427.5 2.8 copy.44
  430.3 3.5 copy.61
  433.9 0.7 all-to-all-done.3
  434.6 0.1 multiply_subtract_fusion
  434.6 0.2 select_reduce_fusion.1
  434.8 0.5 rsqrt_multiply_fusion
  (8 shorter events, 0.1 us)
Async XLA Ops:
  32.8 9.6 %copy-start = (bf16[1024]{0:T(1024)(128)(2,1)S(1)}, bf16[1024]{0:T(1024)(128)(2,1)}, u32[]{:S(2)}) copy-start(bf16[1024]{0:T(1024)(128)(2,1)} %param.9) | copy-start | bytes 6148
  32.8 9.6 %copy-start.2 = (s32[8]{0:T(128)S(1)}, s32[8]{0:T(128)}, u32[]{:S(2)}) copy-start(s32[8]{0:T(128)} %param.7) | copy-start | bytes 100
  32.8 331.7 %all-to-all-start.1 = ((bf16[16,512,1280]{2,1,0:T(8,128)(2,1)}), bf16[16,512,1280]{2,1,0:T(8,128)(2,1)}, u32[]{:S(2)}, u32[]{:S(2)}) async-start(bf16[16,512,1280]{2,1,0:T(8,128)(2,1)} %stack.5), calls=%async_computation.1 | async-start | bytes 41943040 | tf_op jit(solution)/shard_map/all_to_all | solution.py:64
  403.2 9.6 %copy-start.1 = (s32[8,1]{0,1:T(1,128)S(1)}, s32[8,1]{0,1:T(1,128)}, u32[]{:S(2)}) copy-start(s32[8,1]{0,1:T(1,128)} %param.8) | copy-start | bytes 100
  413.6 21.0 %all-to-all-start.3 = ((f32[16,1,48]{2,1,0:T(1,128)}), f32[16,1,48]{2,1,0:T(1,128)S(1)}, u32[]{:S(2)}, u32[]{:S(2)}) async-start(f32[16,1,48]{2,1,0:T(1,128)} %broadcast_in_dim.24), calls=%async_computation.3 | async-start | bytes 16384 | tf_op jit(solution)/shard_map/all_to_all | solution.py:13
